TPU v7x, 32 devices: a whole 2x2x4 slice. The times are simulated.
32 devices in a mesh: leaf: 8 (over y, x, core), group: 4 (over z).
Axes of the slice: x: 2, y: 2, z: 4, core: 2. Of those that a mesh axis runs over, the one named last changes fastest.
Arguments:
- coefficients: float32 [4, 4096, 512], P('group', 'leaf'), may hold values from -6 to 6
- labels: float32 [4, 4096, 512], P('group', 'leaf'), may hold values from -6 to 6
- near_kernel: float32 [4, 4096, 3072], P('group', 'leaf'), may hold values from -0.109375 to 0.109375
- basis: float32 [4, 4096, 256], P('group', 'leaf'), may hold values from -0.1875 to 0.1875
- transfer: float32 [4, 1024, 256], P('group', 'leaf'), may hold values from -0.375 to 0.375
- coupling: float32 [4, 256, 1024], P('group', 'leaf'), may hold values from -0.1875 to 0.1875
- near_lists: int32 [4, 4, 3], P('group'), may hold values from 0 to 3, as said below
- ridge: float32 [1], replicated, may hold values from 0.5 to 2
Outputs:
- residual: float32 [4, 4096, 512], P('group', 'leaf')
Inputs may be any that keep to these rules, and one draw needn't show every extreme that they name: `near_lists`: entry 0 of each leaf's list is the leaf itself; in each group the leaves lie on one cycle through all 4 leaves, and entries 1 and 2 of a leaf's list are its two neighbours on that cycle.
All inputs are finite; a program needn't handle non-finite values.
Results may differ from a plain program's by a relative error of at most 0.0011.
Values may be sent and summed in bfloat16 or wider, within the bound.
No kernel may reach another device: no remote copies, remote signals or barrier semaphores. Data moves between devices by JAX's collectives and lax.ppermute only.
A program may use at most 64 MiB of HBM per device.

v0:
```python
import jax
import jax.numpy as jnp
from jax import lax
from jax.sharding import PartitionSpec as P

LPG = 4


def swapped(shard, axis, distance):
    return lax.ppermute(shard, axis, [(i, i ^ 1 << distance) for i in range(lax.axis_size(axis))])


def matmul(left, right):
    return jnp.dot(left, right, precision=lax.Precision.HIGHEST, preferred_element_type=jnp.float32)


def shards(coefficients, labels, near_kernel, basis, transfer, coupling, near_lists, ridge):
    local_coef = coefficients[0]
    column_count = local_coef.shape[1]
    leaf_split = lax.axis_size("leaf") // LPG
    levels = leaf_split.bit_length() - 1
    position = lax.axis_index("leaf")
    leaf_index = position // leaf_split
    chosen = lax.dynamic_index_in_dim(near_lists[0], leaf_index, 0, keepdims=False)
    local_kernel = near_kernel[0]
    list_length = chosen.shape[0]
    leaf_width = local_kernel.shape[1] // list_length
    group_all = lax.all_gather(coefficients, "leaf", axis=1, tiled=True)[0]
    leaf_blocks = group_all.reshape(group_all.shape[0] // leaf_width, leaf_width, column_count)
    selected = jnp.take(leaf_blocks, chosen, axis=0)
    near = matmul(local_kernel, selected.reshape(list_length * leaf_width, column_count))
    basis_rows = basis[0]
    partial_coef = matmul(basis_rows.T, local_coef)
    for bit_level in reversed(range(levels)):
        halfway = partial_coef.shape[0] // 2
        lower_half = partial_coef[:halfway]
        upper_half = partial_coef[halfway:]
        upper_side = position // (1 << bit_level) % 2 == 1
        kept = jnp.where(upper_side, upper_half, lower_half)
        given = jnp.where(upper_side, lower_half, upper_half)
        partial_coef = kept + swapped(given, "leaf", bit_level)
    contribution = matmul(transfer[0].T, partial_coef)
    coupling_rows = coupling[0]
    group_coef = lax.psum(contribution, "leaf")
    group_round = group_coef.astype(jnp.bfloat16)
    coarse_part = matmul(
        coupling_rows, lax.all_gather(group_round, "group", axis=0, tiled=True).astype(jnp.float32)
    )
    coarse = lax.all_gather(coarse_part, "leaf", axis=0, tiled=True)
    slice_coarse = matmul(transfer[0], coarse)
    for bit_level in range(levels):
        partner = swapped(slice_coarse, "leaf", bit_level)
        upper_side = position // (1 << bit_level) % 2 == 1
        slice_coarse = jnp.where(
            upper_side,
            jnp.concatenate([partner, slice_coarse], axis=0),
            jnp.concatenate([slice_coarse, partner], axis=0),
        )
    far = matmul(basis_rows, slice_coarse)
    result = labels[0] - (near + far + ridge[0] * local_coef)
    return result[None]


def solution(mesh):
    return jax.shard_map(
        shards,
        mesh=mesh,
        in_specs=(
            P("group", "leaf", None),
            P("group", "leaf", None),
            P("group", "leaf", None),
            P("group", "leaf", None),
            P("group", "leaf", None),
            P("group", "leaf", None),
            P("group", None, None),
            P(),
        ),
        out_specs=P("group", "leaf", None),
        check_vma=False,
    )
```

profile of v0, /device:TPU:0, one launch (start us, length us, event | category | flops | bytes accessed | tf_op | source)
XLA Modules:
  0.0 172.0 jit_solution(16874923085528226704)
XLA Ops:
  6.5 0.0 copy-start
  6.5 0.0 copy-start.6
  6.6 0.0 all-gather.5.cloned.1.call-start
  6.6 1.3 copy-done
  7.9 2.3 %fusion.6 = f32[256,512]{1,0:T(8,128)S(1)} fusion(f32[1,512,512]{2,1,0:T(8,128)} %param.8, f32[1,512,256]{2,1,0:T(8,128)S(1)} %copy-done), kind=kOutput, calls=%fused_computation.12 | convolution fusion | flops 805306368 | bytes 2097152 | tf_op jit(solution)/shard_map/dot_general | solution.py:14
  10.3 0.6 collective-permute-start
  10.8 1.2 collective-permute-done
  12.0 1.5 convolution_bitcast_fusion
  13.5 32.9 %all-reduce.1 = bf16[256,512]{0,1:T(8,128)(2,1)} all-reduce(f32[256,512]{0,1:T(8,128)S(1)} %convolution_bitcast_fusion), channel_id=1, replica_groups=mesh['leaf'=8,'group'=4] {'leaf'}, use_global_device_ids=true, to_apply=%region_0.1 | all-reduce | flops 131072 | bytes 786432 | tf_op jit(solution)/shard_map/psum | solution.py:44
  46.4 0.0 all-gather.5.cloned.1.call-update
  46.4 0.0 all-gather.3.cloned.1.call-start
  46.5 0.7 all-gather.3.cloned.1.call-update
  47.2 0.0 copy-done.1
  47.2 1.3 copy.16
  49.2 0.0 copy-done.4
  49.2 1.3 copy.15
  50.5 0.2 dynamic-slice_reduce_fusion
  50.8 25.1 %all-gather.5.cloned.1.call-done = bf16[1024,512]{0,1:T(8,128)(2,1)} async-done(((bf16[256,512]{0,1:T(8,128)(2,1)}), bf16[1024,512]{0,1:T(8,128)(2,1)}) %all-gather.5.cloned.1.call-update) | async-done | bytes 1048592 | tf_op jit(solution)/shard_map/all_gather | solution.py:47
  75.9 2.2 %convolution_bitcast_fusion.2 = f32[32,512]{1,0:T(8,128)S(1)} fusion(bf16[1024,512]{0,1:T(8,128)(2,1)} %all-gather.5.cloned.1.call-done, f32[1,32,1024]{2,1,0:T(8,128)S(1)} %copy-done.6), kind=kOutput, calls=%fused_computation.11 | convolution fusion | flops 201326592 | bytes 1245184 | tf_op jit(solution)/shard_map/dot_general | solution.py:14
  78.1 9.2 %all_gather.11 = f32[256,512]{1,0:T(8,128)S(1)} all-gather(f32[32,512]{1,0:T(8,128)S(1)} %convolution_bitcast_fusion.2), channel_id=1, replica_groups=mesh['leaf'=8,'group'=4] {'leaf'}, dimensions={0}, use_global_device_ids=true | all-gather | bytes 589824 | tf_op jit(solution)/shard_map/all_gather | solution.py:49
  87.3 0.4 convolution_bitcast_fusion.1
  87.8 0.4 collective-permute-start.1
  88.2 42.1 %all-gather.3.cloned.1.call-done = f32[1,4096,512]{2,1,0:T(8,128)} async-done(((f32[1,512,512]{2,1,0:T(8,128)}), f32[1,4096,512]{2,1,0:T(8,128)}) %all-gather.3.cloned.1.call-update) | async-done | bytes 8388624 | tf_op jit(solution)/shard_map/all_gather | solution.py:28
  130.4 7.2 %gather_fusion = f32[3,1024,512]{2,1,0:T(8,128)} fusion(f32[4,1024,512]{2,1,0:T(8,128)} %bitcast.55, s32[1024]{0:T(1024)S(1)} %pad_clamp_fusion), kind=kCustom, calls=%fused_computation | custom fusion | bytes 12582924 | tf_op jit(solution)/shard_map/jit(_take)/gather | solution.py:30
  137.5 3.8 %broadcast_select_fusion = f32[3,1024,512]{2,1,0:T(8,128)S(1)} fusion(f32[3,1024,512]{2,1,0:T(8,128)} %gather_fusion, pred[3]{0:T(512)(128)(4,1)S(1)} %compare_and_fusion), kind=kLoop, calls=%fused_computation.3 | loop fusion | flops 1572864 | bytes 12582915 | tf_op jit(solution)/shard_map/jit(_take)/select_n | solution.py:30
  141.3 0.2 slice-done.1
  141.5 20.3 %fusion = f32[512,512]{1,0:T(8,128)S(1)} fusion(f32[3072,512]{1,0:T(8,128)S(1)} %bitcast.52, f32[1,512,3072]{2,1,0:T(8,128)S(1)} %bitcast.54), kind=kOutput, calls=%fused_computation.1 | convolution fusion | flops 9663676416 | bytes 13631488 | tf_op jit(solution)/shard_map/dot_general | solution.py:14
  161.9 0.0 collective-permute-done.1
  161.9 0.0 copy-done.2
  161.9 0.0 copy-done.3
  161.9 1.9 %fusion.5 = f32[1,512,512]{1,2,0:T(8,128)S(1)} fusion(f32[512,512]{1,0:T(8,128)S(1)} %fusion, f32[1,512,512]{1,2,0:T(8,128)S(1)} %copy-done.2, f32[1,512,512]{1,2,0:T(8,128)S(1)} %copy-done.3, f32[128,512]{1,0:T(8,128)S(1)} %convolution_bitcast_fusion.1, f32[128,512]{1,0:T(8,128)S(1)} %collective-permute-done.1, f32[1,512,256]{2,1,0:T(8,128)S(1)} %copy-done, ...), kind=kOutput, calls=%fused_computation.8 | convolution fusion | flops 806748160 | bytes 5242885 | tf_op jit(solution)/shard_map/dot_general | solution.py:14
  163.8 1.3 copy.17
  (17 shorter events, 0.1 us)
Async XLA Ops:
  6.5 1.4 copy-start
  6.5 40.7 %copy-start.1 = (f32[1,512,512]{2,1,0:T(8,128)S(1)}, f32[1,512,512]{2,1,0:T(8,128)}, u32[]{:S(2)}) copy-start(f32[1,512,512]{2,1,0:T(8,128)} %param.8) | copy-start | bytes 3145732
  6.5 80.8 %copy-start.5 = (f32[1,128,256]{2,1,0:T(8,128)S(1)}, f32[1,128,256]{2,1,0:T(8,128)}, u32[]{:S(2)}) copy-start(f32[1,128,256]{2,1,0:T(8,128)} %param.12) | copy-start | bytes 393220
  6.5 42.6 %copy-start.4 = (f32[1,512,512]{2,1,0:T(8,128)S(1)}, f32[1,512,512]{2,1,0:T(8,128)}, u32[]{:S(2)}) copy-start(f32[1,512,512]{2,1,0:T(8,128)} %param.9) | copy-start | bytes 3145732
  6.5 44.0 %copy-start.7 = (s32[1,4,3]{1,0,2:T(1,128)S(1)}, s32[1,4,3]{1,0,2:T(1,128)}, u32[]{:S(2)}) copy-start(s32[1,4,3]{1,0,2:T(1,128)} %param.14) | copy-start | bytes 148
  6.5 69.3 %copy-start.6 = (f32[1,32,1024]{2,1,0:T(8,128)S(1)}, f32[1,32,1024]{2,1,0:T(8,128)}, u32[]{:S(2)}) copy-start(f32[1,32,1024]{2,1,0:T(8,128)} %param.13) | copy-start | bytes 393220
  6.6 69.3 %all-gather.5.cloned.1.call-start = ((), (), s32[]{:S(2)}) async-start(), calls=%async_computation.1 | async-start | bytes 1310720 | tf_op jit(solution)/shard_map/all_gather | solution.py:47
  10.3 1.7 collective-permute-start
  46.4 83.9 %all-gather.3.cloned.1.call-start = ((), (), s32[]{:S(2)}) async-start(), calls=%async_computation | async-start | bytes 9437184 | tf_op jit(solution)/shard_map/all_gather | solution.py:28
  87.8 74.1 %collective-permute-start.1 = (f32[128,512]{1,0:T(8,128)S(1)}, f32[128,512]{1,0:T(8,128)S(1)}, u32[]{:S(2)}, u32[]{:S(2)}) collective-permute-start(f32[128,512]{1,0:T(8,128)S(1)} %convolution_bitcast_fusion.1), channel_id=1, source_target_pairs={{0,4},{4,0},{8,12},{12,8},{16,20},{20,16},{24,28},{28,24},{1,5},{5... | collective-permute-start | bytes 786440 | tf_op jit(solution)/shard_map/ppermute | solution.py:10
  130.4 11.0 %slice-start = ((s8[6291456]{0:T(1024)(128)(4,1)}), s8[2097152]{0:T(1024)(128)(4,1)S(1)}, s32[]{:S(2)}) async-start(s8[6291456]{0:T(1024)(128)(4,1)} %bitcast.53), calls=%async_computation.2 | async-start | bytes 4194304
  137.5 4.0 %slice-start.1 = ((s8[6291456]{0:T(1024)(128)(4,1)}), s8[4194304]{0:T(1024)(128)(4,1)S(1)}, s32[]{:S(2)}) async-start(s8[6291456]{0:T(1024)(128)(4,1)} %bitcast.53), calls=%async_computation.3 | async-start | bytes 8388608
  141.5 20.3 %copy-start.2 = (f32[1,512,512]{1,2,0:T(8,128)S(1)}, f32[1,512,512]{1,2,0:T(8,128)}, u32[]{:S(2)}) copy-start(f32[1,512,512]{1,2,0:T(8,128)} %copy.16) | copy-start | bytes 3145732
  141.5 20.4 %copy-start.3 = (f32[1,512,512]{1,2,0:T(8,128)S(1)}, f32[1,512,512]{1,2,0:T(8,128)}, u32[]{:S(2)}) copy-start(f32[1,512,512]{1,2,0:T(8,128)} %copy.15) | copy-start | bytes 3145732
Sparse Core Ops, SparseCore 0:
  46.6 29.2 all-gather.4
  77.8 52.5 all-gather.2
where the time goes:
time: 172 us
  waiting for transfers between devices  69.1 us (40%)
  blocking collectives  42.1 us (24%)
  matrix products  28.7 us (17%)
  between operations  14.2 us (8%)
  local copies, waits for them, and re-layouts  12.9 us (8%)
  other arithmetic  3.85 us (2%)
    all_gather x1, waiting for transfers between devices, shards(): group_all = lax.all_gather(coefficients, 'leaf', axis=1, tiled=True)[0]  42.1 us
    psum x1, blocking collectives, shards(): group_coef = lax.psum(contribution, 'leaf')  32.9 us
    dot_general x6, matrix products, matmul(): jnp.dot(left, right, precision=lax.Precision.HIGHEST, preferred_element_t...  28.7 us
    all_gather x1, waiting for transfers between devices, shards(): lax.all_gather(group_round, 'group', axis=0, tiled=True).astype(jnp.float32)  25.1 us
    all_gather x1, blocking collectives, shards(): coarse = lax.all_gather(coarse_part, 'leaf', axis=0, tiled=True)  9.22 us
    gather x1, local copies, waits for them, and re-layouts, shards(): selected = jnp.take(leaf_blocks, chosen, axis=0)  7.17 us
    unnamed x22, local copies, waits for them, and re-layouts  4.18 us
    select_n x2, other arithmetic, shards(): selected = jnp.take(leaf_blocks, chosen, axis=0)  3.8 us
  transfers between devices with their start and end apart: 4, of which 3 were waited for; matrix products, arithmetic and copies ran while one was open for 21% of the time, Pallas kernels for 0%

commit v1 on v0

--- a/solution.py
+++ b/solution.py
@@ -41,7 +41,7 @@
         partial_coef = kept + swapped(given, "leaf", bit_level)
     contribution = matmul(transfer[0].T, partial_coef)
     coupling_rows = coupling[0]
-    group_coef = lax.psum(contribution, "leaf")
+    group_coef = jnp.sum(lax.all_gather(contribution, "leaf"), axis=0)
     group_round = group_coef.astype(jnp.bfloat16)
     coarse_part = matmul(
         coupling_rows, lax.all_gather(group_round, "group", axis=0, tiled=True).astype(jnp.float32)

time: 172 us -> 187 us (1.087)
  waiting for transfers between devices: 69.1 us -> 110 us
  blocking collectives: 42.1 us -> 9.22 us
  local copies, waits for them, and re-layouts: 12.9 us -> 16.9 us
  other arithmetic: 3.85 us -> 5.84 us
    all_gather x0 -> x1, waiting for transfers between devices: none -> 40.1 us  [shards(): group_coef = jnp.sum(lax.all_gather(contribution, 'leaf'), axis=0)]
    psum x1 -> x0, blocking collectives: 32.9 us -> none  [shards(): group_coef = lax.psum(contribution, 'leaf')]
    unnamed x22 -> x23, local copies, waits for them, and re-layouts: 4.18 us -> 8.19 us
    reduce_sum x0 -> x1, other arithmetic: none -> 2 us  [shards(): group_coef = jnp.sum(lax.all_gather(contribution, 'leaf'), axis=0)]
  transfers between devices with their start and end apart: 4 -> 5, of which waited for: 3 -> 4; matrix products, arithmetic and copies ran while one was open for 21% -> 20% of each run, Pallas kernels for 0% -> 0%
where the time goes in v1:
time: 187 us; the launch traced here: 186 us
  waiting for transfers between devices  110 us (59%)
  matrix products  29.5 us (16%)
  local copies, waits for them, and re-layouts  16.9 us (9%)
  between operations  13.9 us (7%)
  blocking collectives  9.22 us (5%)
  other arithmetic  5.84 us (3%)
    all_gather x1, waiting for transfers between devices, shards(): group_all = lax.all_gather(coefficients, 'leaf', axis=1, tiled=True)[0]  42.1 us
    all_gather x1, waiting for transfers between devices, shards(): group_coef = jnp.sum(lax.all_gather(contribution, 'leaf'), axis=0)  40.1 us
    dot_general x6, matrix products, matmul(): jnp.dot(left, right, precision=lax.Precision.HIGHEST, preferred_element_t...  29.5 us
    all_gather x1, waiting for transfers between devices, shards(): lax.all_gather(group_round, 'group', axis=0, tiled=True).astype(jnp.float32)  25.8 us
    all_gather x1, blocking collectives, shards(): coarse = lax.all_gather(coarse_part, 'leaf', axis=0, tiled=True)  9.22 us
    unnamed x23, local copies, waits for them, and re-layouts  8.19 us
    gather x1, local copies, waits for them, and re-layouts, shards(): selected = jnp.take(leaf_blocks, chosen, axis=0)  7.18 us
    select_n x2, other arithmetic, shards(): selected = jnp.take(leaf_blocks, chosen, axis=0)  3.8 us
  transfers between devices with their start and end apart: 5, of which 4 were waited for; matrix products, arithmetic and copies ran while one was open for 20% of the time, Pallas kernels for 0%

profile of v1, /device:TPU:0, one launch (start us, length us, event | category | flops | bytes accessed | tf_op | source)
XLA Modules:
  0.0 186.3 jit_solution(14999747037506975875)
XLA Ops:
  6.5 1.0 copy-done
  7.6 2.3 %fusion.6 = f32[256,512]{1,0:T(8,128)S(1)} fusion(f32[1,512,512]{2,1,0:T(8,128)} %param.8, f32[1,512,256]{2,1,0:T(8,128)S(1)} %copy-done), kind=kOutput, calls=%fused_computation.13 | convolution fusion | flops 805306368 | bytes 2097152 | tf_op jit(solution)/shard_map/dot_general | solution.py:14
  9.9 0.6 collective-permute-start
  10.5 1.2 collective-permute-done
  11.6 2.3 %convolution_bitcast_fusion = f32[256,512]{0,1:T(8,128)} fusion(f32[128,512]{1,0:T(8,128)S(1)} %collective-permute-done, f32[256,512]{1,0:T(8,128)S(1)} %fusion.6, f32[1,128,256]{2,1,0:T(8,128)} %param.12, pred[]{:T(512)S(6)} %eq.7), kind=kOutput, calls=%fused_computation.10 | convolution fusion | flops 201457664 | bytes 1441793 | tf_op jit(solution)/shard_map/dot_general | solution.py:14
  14.0 0.0 all-gather.9.cloned.1.call-update
  14.0 0.0 all-gather.7.cloned.1.call-start
  14.0 40.1 %all-gather.9.cloned.1.call-done = f32[2048,512]{0,1:T(8,128)} async-done(((f32[256,512]{0,1:T(8,128)}), f32[2048,512]{0,1:T(8,128)}) %all-gather.9.cloned.1.call-update) | async-done | bytes 4194320 | tf_op jit(solution)/shard_map/all_gather | solution.py:44
  54.1 4.3 %copy.18 = f32[64,8,8,256]{3,2,1,0:T(8,128)S(1)} copy(f32[64,8,8,256]{3,1,2,0:T(8,128)} %bitcast.61) | data formatting | bytes 8388608
  58.4 0.0 copy-start.7
  58.4 0.0 copy-start.6
  58.4 0.0 copy-start.5
  58.4 2.0 %bitcast_reduce_fusion = bf16[256,512]{0,1:T(8,128)(2,1)} fusion(f32[64,8,8,256]{3,2,1,0:T(8,128)S(1)} %copy.18), kind=kLoop, calls=%fused_computation.3 | loop fusion | flops 917504 | bytes 4456448 | tf_op jit(solution)/shard_map/reduce_sum | solution.py:44
  60.4 0.0 all-gather.7.cloned.1.call-update
  60.4 0.0 all-gather.5.cloned.1.call-start
  60.5 0.7 all-gather.5.cloned.1.call-update
  61.2 1.3 copy.16
  63.2 1.3 copy.15
  64.5 0.2 dynamic-slice_reduce_fusion
  64.8 25.8 %all-gather.7.cloned.1.call-done = bf16[1024,512]{0,1:T(8,128)(2,1)} async-done(((bf16[256,512]{0,1:T(8,128)(2,1)}), bf16[1024,512]{0,1:T(8,128)(2,1)}) %all-gather.7.cloned.1.call-update) | async-done | bytes 1048592 | tf_op jit(solution)/shard_map/all_gather | solution.py:47
  90.5 2.2 %convolution_bitcast_fusion.2 = f32[32,512]{1,0:T(8,128)S(1)} fusion(bf16[1024,512]{0,1:T(8,128)(2,1)} %all-gather.7.cloned.1.call-done, f32[1,32,1024]{2,1,0:T(8,128)S(1)} %copy-done.6), kind=kOutput, calls=%fused_computation.12 | convolution fusion | flops 201326592 | bytes 1245184 | tf_op jit(solution)/shard_map/dot_general | solution.py:14
  92.8 9.2 %all_gather.19 = f32[256,512]{1,0:T(8,128)S(1)} all-gather(f32[32,512]{1,0:T(8,128)S(1)} %convolution_bitcast_fusion.2), channel_id=1, replica_groups=mesh['leaf'=8,'group'=4] {'leaf'}, dimensions={0}, use_global_device_ids=true | all-gather | bytes 589824 | tf_op jit(solution)/shard_map/all_gather | solution.py:49
  102.0 0.4 convolution_bitcast_fusion.1
  102.4 0.4 collective-permute-start.1
  102.9 42.1 %all-gather.5.cloned.1.call-done = f32[1,4096,512]{2,1,0:T(8,128)} async-done(((f32[1,512,512]{2,1,0:T(8,128)}), f32[1,4096,512]{2,1,0:T(8,128)}) %all-gather.5.cloned.1.call-update) | async-done | bytes 8388624 | tf_op jit(solution)/shard_map/all_gather | solution.py:28
  145.0 7.2 %gather_fusion = f32[3,1024,512]{2,1,0:T(8,128)} fusion(f32[4,1024,512]{2,1,0:T(8,128)} %bitcast.60, s32[1024]{0:T(1024)S(1)} %pad_clamp_fusion), kind=kCustom, calls=%fused_computation | custom fusion | bytes 12582924 | tf_op jit(solution)/shard_map/jit(_take)/gather | solution.py:30
  152.2 3.8 %broadcast_select_fusion = f32[3,1024,512]{2,1,0:T(8,128)S(1)} fusion(f32[3,1024,512]{2,1,0:T(8,128)} %gather_fusion, pred[3]{0:T(512)(128)(4,1)S(1)} %compare_and_fusion), kind=kLoop, calls=%fused_computation.4 | loop fusion | flops 1572864 | bytes 12582915 | tf_op jit(solution)/shard_map/jit(_take)/select_n | solution.py:30
  156.0 0.2 slice-done.1
  156.2 20.3 %fusion = f32[512,512]{1,0:T(8,128)S(1)} fusion(f32[3072,512]{1,0:T(8,128)S(1)} %bitcast.57, f32[1,512,3072]{2,1,0:T(8,128)S(1)} %bitcast.59), kind=kOutput, calls=%fused_computation.1 | convolution fusion | flops 9663676416 | bytes 13631488 | tf_op jit(solution)/shard_map/dot_general | solution.py:14
  176.5 0.0 collective-permute-done.1
  176.6 1.9 %fusion.5 = f32[1,512,512]{1,2,0:T(8,128)S(1)} fusion(f32[512,512]{1,0:T(8,128)S(1)} %fusion, f32[1,512,512]{1,2,0:T(8,128)S(1)} %copy-done.2, f32[1,512,512]{1,2,0:T(8,128)S(1)} %copy-done.3, f32[128,512]{1,0:T(8,128)S(1)} %convolution_bitcast_fusion.1, f32[128,512]{1,0:T(8,128)S(1)} %collective-permute-done.1, f32[1,512,256]{2,1,0:T(8,128)S(1)} %copy-done, ...), kind=kOutput, calls=%fused_computation.9 | convolution fusion | flops 806748160 | bytes 5242885 | tf_op jit(solution)/shard_map/dot_general | solution.py:14
  178.5 1.3 copy.17
  (21 shorter events, 0.1 us)
Async XLA Ops:
  6.5 1.0 copy-start
  6.5 47.5 %all-gather.9.cloned.1.call-start = ((), (), s32[]{:S(2)}) async-start(), calls=%async_computation.2 | async-start | bytes 4718592 | tf_op jit(solution)/shard_map/all_gather | solution.py:44
  9.9 1.7 collective-permute-start
  14.0 76.5 %all-gather.7.cloned.1.call-start = ((), (), s32[]{:S(2)}) async-start(), calls=%async_computation.1 | async-start | bytes 1310720 | tf_op jit(solution)/shard_map/all_gather | solution.py:47
  54.1 7.1 %copy-start.1 = (f32[1,512,512]{2,1,0:T(8,128)S(1)}, f32[1,512,512]{2,1,0:T(8,128)}, u32[]{:S(2)}) copy-start(f32[1,512,512]{2,1,0:T(8,128)} %param.8) | copy-start | bytes 3145732
  54.1 9.1 %copy-start.4 = (f32[1,512,512]{2,1,0:T(8,128)S(1)}, f32[1,512,512]{2,1,0:T(8,128)}, u32[]{:S(2)}) copy-start(f32[1,512,512]{2,1,0:T(8,128)} %param.9) | copy-start | bytes 3145732
  58.4 6.1 %copy-start.7 = (s32[1,4,3]{1,0,2:T(1,128)S(1)}, s32[1,4,3]{1,0,2:T(1,128)}, u32[]{:S(2)}) copy-start(s32[1,4,3]{1,0,2:T(1,128)} %param.14) | copy-start | bytes 148
  58.4 32.1 %copy-start.6 = (f32[1,32,1024]{2,1,0:T(8,128)S(1)}, f32[1,32,1024]{2,1,0:T(8,128)}, u32[]{:S(2)}) copy-start(f32[1,32,1024]{2,1,0:T(8,128)} %param.13) | copy-start | bytes 393220
  58.4 43.6 %copy-start.5 = (f32[1,128,256]{2,1,0:T(8,128)S(1)}, f32[1,128,256]{2,1,0:T(8,128)}, u32[]{:S(2)}) copy-start(f32[1,128,256]{2,1,0:T(8,128)} %param.12) | copy-start | bytes 393220
  60.4 84.6 %all-gather.5.cloned.1.call-start = ((), (), s32[]{:S(2)}) async-start(), calls=%async_computation | async-start | bytes 9437184 | tf_op jit(solution)/shard_map/all_gather | solution.py:28
  102.4 74.1 %collective-permute-start.1 = (f32[128,512]{1,0:T(8,128)S(1)}, f32[128,512]{1,0:T(8,128)S(1)}, u32[]{:S(2)}, u32[]{:S(2)}) collective-permute-start(f32[128,512]{1,0:T(8,128)S(1)} %convolution_bitcast_fusion.1), channel_id=1, source_target_pairs={{0,4},{4,0},{8,12},{12,8},{16,20},{20,16},{24,28},{28,24},{1,5},{5... | collective-permute-start | bytes 786440 | tf_op jit(solution)/shard_map/ppermute | solution.py:10
  145.0 11.0 %slice-start = ((s8[6291456]{0:T(1024)(128)(4,1)}), s8[2097152]{0:T(1024)(128)(4,1)S(1)}, s32[]{:S(2)}) async-start(s8[6291456]{0:T(1024)(128)(4,1)} %bitcast.58), calls=%async_computation.3 | async-start | bytes 4194304
  152.2 4.0 %slice-start.1 = ((s8[6291456]{0:T(1024)(128)(4,1)}), s8[4194304]{0:T(1024)(128)(4,1)S(1)}, s32[]{:S(2)}) async-start(s8[6291456]{0:T(1024)(128)(4,1)} %bitcast.58), calls=%async_computation.4 | async-start | bytes 8388608
  156.2 20.3 %copy-start.2 = (f32[1,512,512]{1,2,0:T(8,128)S(1)}, f32[1,512,512]{1,2,0:T(8,128)}, u32[]{:S(2)}) copy-start(f32[1,512,512]{1,2,0:T(8,128)} %copy.16) | copy-start | bytes 3145732
  156.2 20.4 %copy-start.3 = (f32[1,512,512]{1,2,0:T(8,128)S(1)}, f32[1,512,512]{1,2,0:T(8,128)}, u32[]{:S(2)}) copy-start(f32[1,512,512]{1,2,0:T(8,128)} %copy.15) | copy-start | bytes 3145732
Sparse Core Ops, SparseCore 0:
  14.1 39.9 all-gather.8
  60.6 29.9 all-gather.6
  92.4 52.5 all-gather.4
